TPU v7x, 512 devices: a whole 4x4x16 slice. The times are simulated.
512 devices in a mesh: box: 16 (over z), row: 4 (over y_hi, core), col: 8 (over x, y_lo).
Axes of the slice: x: 4, y: 4 (y_hi: 2, y_lo: 2; y = y_hi * 2 + y_lo), z: 16, core: 2. Of those that a mesh axis runs over, the one named last changes fastest.
Arguments:
- ext_ext: float32 [16, 3072, 3072], P('box', 'row', 'col'), may hold values from -6 to 6
- ext_int: float32 [16, 3072, 1024], P('box', 'row', 'col'), may hold values from -0.1875 to 0.1875
- int_ext: float32 [16, 1024, 3072], P('box', 'row', 'col'), may hold values from -6 to 6
- int_int: float32 [16, 1024, 1024], P('box', 'row', 'col'), may hold values from -0.1 to 0.1, as said below
Outputs:
- merged: float32 [16, 3072, 2, 3072], P('box', 'row', None, 'col')
Inputs may be any that keep to these rules, and one draw needn't show every extreme that they name: `int_int`: independent entries.
All inputs are finite; a program needn't handle non-finite values.
Results may differ from a plain program's by a relative error of at most 0.0003.
Values sent between devices are 32-bit elements; how exact they have to be, the bound alone decides.
A program may use at most 64 MiB of HBM per device.

v0:
```python
import jax
import jax.numpy as jnp
from jax import lax
from jax.sharding import PartitionSpec as P

HIGH = lax.Precision.HIGHEST


def in_order(pieces, dim):
    pieces = jnp.moveaxis(pieces, 0, dim)
    dims = pieces.shape
    return pieces.reshape(*dims[:dim], dims[dim] * dims[dim + 1], *dims[dim + 2 :])


def sent_to_all(shard, axis):
    devices = lax.axis_size(axis)
    return lax.all_to_all(
        jnp.broadcast_to(shard[None], (devices, *shard.shape)), axis, 0, 0, tiled=True
    )


def gathered_copies(shard, axis, dim):
    return in_order(sent_to_all(shard, axis), dim)


def swapped(shard, axis, distance):
    return lax.ppermute(shard, axis, [(i, i ^ 1 << distance) for i in range(lax.axis_size(axis))])


def panel_dot(total, piece, panel):
    return total + jnp.dot(piece, panel, precision=HIGH, preferred_element_type=jnp.float32)


def chain_product(left, right):
    panel = gathered_copies(right, "row", 0)
    empty = jnp.zeros((left.shape[0], right.shape[1]), jnp.float32)
    return panel_dot(empty, gathered_copies(left, "col", 1), panel)


def local(ext_ext, ext_int, int_ext, int_int):
    own_ee = ext_ext[0]
    own_ed = ext_int[0]
    own_de = int_ext[0]
    own_dd = int_int[0]
    partner_dd, partner_de = swapped((own_dd, own_de), "box", 0)
    is_even = lax.axis_index("box") % 2 == 0
    block_rows = own_dd.shape[0]
    block_cols = own_dd.shape[1]
    row_ids = lax.axis_index("row") * block_rows + lax.broadcasted_iota(
        jnp.int32, (block_rows, block_cols), 0
    )
    col_ids = lax.axis_index("col") * block_cols + lax.broadcasted_iota(
        jnp.int32, (block_rows, block_cols), 1
    )
    identity = (row_ids == col_ids).astype(jnp.float32)
    coupling = chain_product(partner_dd, own_dd)
    square = chain_product(coupling, coupling)
    first = identity + coupling
    inverse = first + chain_product(first, square)
    de_panel = gathered_copies(own_de, "row", 0)
    coupled = panel_dot(
        jnp.zeros(own_de.shape, jnp.float32), gathered_copies(partner_dd, "col", 1), de_panel
    )
    source = jnp.concatenate(
        [jnp.where(is_even, coupled, partner_de), jnp.where(is_even, partner_de, coupled)], axis=1
    )
    source_panel = lax.all_gather(source, "row", axis=0, tiled=True)
    carried = panel_dot(
        jnp.zeros(source.shape, jnp.float32), gathered_copies(inverse, "col", 1), source_panel
    )
    right_panel = lax.all_gather(carried, "row", axis=0, tiled=True)
    zeros = jnp.zeros_like(own_ee)
    start_terms = jnp.concatenate(
        [jnp.where(is_even, own_ee, zeros), jnp.where(is_even, zeros, own_ee)], axis=1
    )
    merged = panel_dot(start_terms, lax.all_gather(own_ed, "col", axis=1, tiled=True), right_panel)
    return merged.reshape(1, own_ee.shape[0], 2, own_ee.shape[1])


def solution(mesh):
    placed = (
        P("box", "row", "col"),
        P("box", "row", "col"),
        P("box", "row", "col"),
        P("box", "row", "col"),
    )
    return jax.shard_map(
        local, mesh=mesh, in_specs=placed, out_specs=P("box", "row", None, "col"), check_vma=False
    )
```

profile of v0, /device:TPU:1, one launch (start us, length us, event | category | flops | bytes accessed | tf_op | source)
XLA Modules:
  0.0 298.8 jit_solution(4053123968927167016)
XLA Ops:
  6.5 4.5 %collective-permute-start = (f32[256,128]{1,0:T(8,128)}, f32[256,128]{1,0:T(8,128)S(1)}, u32[]{:S(2)}, u32[]{:S(2)}) collective-permute-start(f32[256,128]{1,0:T(8,128)} %bitcast.53), channel_id=1, source_target_pairs={{0,32},{32,0},{64,96},{96,64},{128,160},{160,128},{192,224},{224,1... | collective-permute-start | bytes 393224 | tf_op jit(solution)/shard_map/ppermute | solution.py:27
  11.0 2.6 collective-permute-done
  13.8 17.0 %all_to_all.41 = f32[8,256,128]{1,2,0:T(8,128)S(1)} all-to-all(f32[8,256,128]{1,2,0:T(8,128)S(1)} %broadcast_in_dim.21), channel_id=1, replica_groups=mesh['box'=16,'row'=4,'col'=8] {'col'}, dimensions={0} | all-to-all | bytes 2097152 | tf_op jit(solution)/shard_map/all_to_all | solution.py:17
  30.8 1.2 broadcast_in_dim.29
  32.0 9.1 %all-to-all-start.7 = ((f32[4,256,384]{2,1,0:T(8,128)}), f32[4,256,384]{2,1,0:T(8,128)S(1)}, u32[]{:S(2)}, u32[]{:S(2)}) async-start(f32[4,256,384]{2,1,0:T(8,128)} %broadcast_in_dim.29), calls=%async_computation.7 | async-start | bytes 3145728 | tf_op jit(solution)/shard_map/all_to_all | solution.py:17
  41.1 3.2 %collective-permute-start.1 = (f32[256,384]{1,0:T(8,128)S(1)}, f32[256,384]{1,0:T(8,128)S(1)}, u32[]{:S(2)}, u32[]{:S(2)}) collective-permute-start(f32[256,384]{1,0:T(8,128)S(1)} %bitcast.52), channel_id=1, source_target_pairs={{0,32},{32,0},{64,96},{96,64},{128,160},{160,128},{192,224},{224,1... | collective-permute-start | bytes 1179656 | tf_op jit(solution)/shard_map/ppermute | solution.py:27
  44.3 9.4 %collective-permute-done.1 = f32[256,384]{1,0:T(8,128)S(1)} collective-permute-done((f32[256,384]{1,0:T(8,128)S(1)}, f32[256,384]{1,0:T(8,128)S(1)}, u32[]{:S(2)}, u32[]{:S(2)}) %collective-permute-start.1) | collective-permute-done | bytes 393248 | tf_op jit(solution)/shard_map/ppermute | solution.py:27
  53.6 8.0 %all-to-all-done.7 = f32[4,256,384]{2,1,0:T(8,128)S(1)} async-done(((f32[4,256,384]{2,1,0:T(8,128)}), f32[4,256,384]{2,1,0:T(8,128)S(1)}, u32[]{:S(2)}, u32[]{:S(2)}) %all-to-all-start.7) | async-done | bytes 1572896 | tf_op jit(solution)/shard_map/all_to_all | solution.py:17
  61.7 1.9 broadcast_select_fusion.1
  63.5 0.9 pad_maximum_fusion
  65.3 0.8 broadcast_in_dim.22
  66.1 4.4 %all-to-all-start.1 = ((f32[4,256,128]{2,1,0:T(8,128)}), f32[4,256,128]{2,1,0:T(8,128)S(1)}, u32[]{:S(2)}, u32[]{:S(2)}) async-start(f32[4,256,128]{2,1,0:T(8,128)} %broadcast_in_dim.22), calls=%async_computation.1 | async-start | bytes 1048576 | tf_op jit(solution)/shard_map/all_to_all | solution.py:17
  70.5 9.3 %all-to-all-done.1 = f32[4,256,128]{2,1,0:T(8,128)S(1)} async-done(((f32[4,256,128]{2,1,0:T(8,128)}), f32[4,256,128]{2,1,0:T(8,128)S(1)}, u32[]{:S(2)}, u32[]{:S(2)}) %all-to-all-start.1) | async-done | bytes 524320 | tf_op jit(solution)/shard_map/all_to_all | solution.py:17
  79.9 1.8 convert_add_fusion
  82.5 4.4 %all-to-all-start.4 = ((f32[4,256,128]{2,1,0:T(8,128)}), f32[4,256,128]{2,1,0:T(8,128)S(1)}, u32[]{:S(2)}, u32[]{:S(2)}) async-start(f32[4,256,128]{2,1,0:T(8,128)} %broadcast_in_dim.25), calls=%async_computation.4 | async-start | bytes 1048576 | tf_op jit(solution)/shard_map/all_to_all | solution.py:17
  87.0 15.5 %all-to-all-done.4 = f32[4,256,128]{2,1,0:T(8,128)S(1)} async-done(((f32[4,256,128]{2,1,0:T(8,128)}), f32[4,256,128]{2,1,0:T(8,128)S(1)}, u32[]{:S(2)}, u32[]{:S(2)}) %all-to-all-start.4) | async-done | bytes 524320 | tf_op jit(solution)/shard_map/all_to_all | solution.py:17
  102.5 1.1 broadcast_in_dim.24
  103.6 3.6 %all-to-all-start.3 = ((f32[8,256,128]{1,2,0:T(8,128)}), f32[8,256,128]{1,2,0:T(8,128)S(1)}, u32[]{:S(2)}, u32[]{:S(2)}) async-start(f32[8,256,128]{1,2,0:T(8,128)} %broadcast_in_dim.24), calls=%async_computation.3 | async-start | bytes 2097152 | tf_op jit(solution)/shard_map/all_to_all | solution.py:17
  107.3 15.4 %all-to-all-done.3 = f32[8,256,128]{1,2,0:T(8,128)S(1)} async-done(((f32[8,256,128]{1,2,0:T(8,128)}), f32[8,256,128]{1,2,0:T(8,128)S(1)}, u32[]{:S(2)}, u32[]{:S(2)}) %all-to-all-start.3) | async-done | bytes 1048608 | tf_op jit(solution)/shard_map/all_to_all | solution.py:17
  122.7 1.1 broadcast_in_dim.23
  123.8 3.6 %all-to-all-start.2 = ((f32[8,256,128]{1,2,0:T(8,128)}), f32[8,256,128]{1,2,0:T(8,128)S(1)}, u32[]{:S(2)}, u32[]{:S(2)}) async-start(f32[8,256,128]{1,2,0:T(8,128)} %broadcast_in_dim.23), calls=%async_computation.2 | async-start | bytes 2097152 | tf_op jit(solution)/shard_map/all_to_all | solution.py:17
  127.4 1.8 fusion.4
  129.2 16.9 %all-to-all-done.2 = f32[8,256,128]{1,2,0:T(8,128)S(1)} async-done(((f32[8,256,128]{1,2,0:T(8,128)}), f32[8,256,128]{1,2,0:T(8,128)S(1)}, u32[]{:S(2)}, u32[]{:S(2)}) %all-to-all-start.2) | async-done | bytes 1048608 | tf_op jit(solution)/shard_map/all_to_all | solution.py:17
  146.1 20.6 %all_to_all.42 = f32[4,256,128]{2,1,0:T(8,128)S(1)} all-to-all(f32[4,256,128]{2,1,0:T(8,128)S(1)} %broadcast_in_dim.26), channel_id=1, replica_groups=mesh['box'=16,'row'=4,'col'=8] {'row'}, dimensions={0} | all-to-all | bytes 1048576 | tf_op jit(solution)/shard_map/all_to_all | solution.py:17
  166.8 1.8 convolution_add_fusion
  168.8 31.7 %all_to_all.43 = f32[8,256,128]{1,2,0:T(8,128)S(1)} all-to-all(f32[8,256,128]{1,2,0:T(8,128)S(1)} %broadcast_in_dim.27), channel_id=1, replica_groups=mesh['box'=16,'row'=4,'col'=8] {'col'}, dimensions={0} | all-to-all | bytes 2097152 | tf_op jit(solution)/shard_map/all_to_all | solution.py:17
  200.5 5.7 %fusion.5 = f32[256,768]{1,0:T(8,128)} fusion(f32[256,1024]{0,1:T(8,128)S(1)} %bitcast.45, f32[1024,768]{1,0:T(8,128)} %all-gather.5.cloned.1.call-done), kind=kOutput, calls=%fused_computation.13 | convolution fusion | flops 2415919104 | bytes 4980736 | tf_op jit(solution)/shard_map/dot_general | solution.py:31
  206.6 1.2 select_bitcast_fusion.1
  207.8 9.9 %all-gather.9.cloned.1.call-done = f32[1,768,1024]{2,1,0:T(8,128)} async-done(((f32[1,768,128]{2,1,0:T(8,128)}), f32[1,768,1024]{2,1,0:T(8,128)}) %all-gather.9.cloned.1.call-update) | async-done | bytes 3145744 | tf_op jit(solution)/shard_map/all_gather | solution.py:76
  217.6 54.1 %all-gather.7.cloned.1.call-done = f32[1024,768]{1,0:T(8,128)} async-done(((f32[256,768]{1,0:T(8,128)}), f32[1024,768]{1,0:T(8,128)}) %all-gather.7.cloned.1.call-update) | async-done | bytes 3145744 | tf_op jit(solution)/shard_map/all_gather | solution.py:71
  271.7 17.5 %maximum_add_fusion = f32[768,768]{0,1:T(8,128)S(1)} fusion(f32[768,384]{0,1:T(8,128)} %get-tuple-element.6, f32[768,384]{0,1:T(8,128)S(1)} %get-tuple-element.5, f32[1024,768]{1,0:T(8,128)} %all-gather.7.cloned.1.call-done, f32[1,768,1024]{2,1,0:T(8,128)} %all-gather.9.cloned.1.call-done), kind=kOutput, calls=%fused_computation.2 | convolution fusion | flops 7248936960 | bytes 11010048 | tf_op jit(solution)/shard_map/dot_general | solution.py:31
  289.2 3.0 %copy.14 = f32[1,768,2,384]{3,2,1,0:T(2,128)} copy(f32[1,768,2,384]{1,3,2,0:T(8,128)S(1)} %bitcast.41) | data formatting | bytes 4718592 | tf_op jit(solution)/shard_map/reshape | solution.py:77
  (24 shorter events, 2.6 us)
Async XLA Ops:
  6.5 24.2 %copy-start.1 = (f32[1,256,384]{2,1,0:T(8,128)S(1)}, f32[1,256,384]{2,1,0:T(8,128)}, u32[]{:S(2)}) copy-start(f32[1,256,384]{2,1,0:T(8,128)} %param.6) | copy-start | bytes 1179652
  6.5 7.0 %collective-permute-start = (f32[256,128]{1,0:T(8,128)}, f32[256,128]{1,0:T(8,128)S(1)}, u32[]{:S(2)}, u32[]{:S(2)}) collective-permute-start(f32[256,128]{1,0:T(8,128)} %bitcast.53), channel_id=1, source_target_pairs={{0,32},{32,0},{64,96},{96,64},{128,160},{160,128},{192,224},{224,1... | collective-permute-start | bytes 393224 | tf_op jit(solution)/shard_map/ppermute | solution.py:27
  32.0 29.6 %all-to-all-start.7 = ((f32[4,256,384]{2,1,0:T(8,128)}), f32[4,256,384]{2,1,0:T(8,128)S(1)}, u32[]{:S(2)}, u32[]{:S(2)}) async-start(f32[4,256,384]{2,1,0:T(8,128)} %broadcast_in_dim.29), calls=%async_computation.7 | async-start | bytes 3145728 | tf_op jit(solution)/shard_map/all_to_all | solution.py:17
  41.1 159.4 %all-gather.5.cloned.1.call-start = ((), (), s32[]{:S(2)}) async-start(), calls=%async_computation.8 | async-start | bytes 3932160 | tf_op jit(solution)/shard_map/all_gather | solution.py:67
  41.1 12.6 %collective-permute-start.1 = (f32[256,384]{1,0:T(8,128)S(1)}, f32[256,384]{1,0:T(8,128)S(1)}, u32[]{:S(2)}, u32[]{:S(2)}) collective-permute-start(f32[256,384]{1,0:T(8,128)S(1)} %bitcast.52), channel_id=1, source_target_pairs={{0,32},{32,0},{64,96},{96,64},{128,160},{160,128},{192,224},{224,1... | collective-permute-start | bytes 1179656 | tf_op jit(solution)/shard_map/ppermute | solution.py:27
  61.7 3.6 %copy-start.2 = (f32[1,256,128]{2,1,0:T(8,128)S(1)}, f32[1,256,128]{2,1,0:T(8,128)}, u32[]{:S(2)}) copy-start(f32[1,256,128]{2,1,0:T(8,128)} %param.7) | copy-start | bytes 393220
  64.5 153.1 %all-gather.9.cloned.1.call-start = ((), (), s32[]{:S(2)}) async-start(), calls=%async_computation.10 | async-start | bytes 3538944 | tf_op jit(solution)/shard_map/all_gather | solution.py:76
  66.1 13.8 %all-to-all-start.1 = ((f32[4,256,128]{2,1,0:T(8,128)}), f32[4,256,128]{2,1,0:T(8,128)S(1)}, u32[]{:S(2)}, u32[]{:S(2)}) async-start(f32[4,256,128]{2,1,0:T(8,128)} %broadcast_in_dim.22), calls=%async_computation.1 | async-start | bytes 1048576 | tf_op jit(solution)/shard_map/all_to_all | solution.py:17
  82.5 20.1 %all-to-all-start.4 = ((f32[4,256,128]{2,1,0:T(8,128)}), f32[4,256,128]{2,1,0:T(8,128)S(1)}, u32[]{:S(2)}, u32[]{:S(2)}) async-start(f32[4,256,128]{2,1,0:T(8,128)} %broadcast_in_dim.25), calls=%async_computation.4 | async-start | bytes 1048576 | tf_op jit(solution)/shard_map/all_to_all | solution.py:17
  103.6 19.1 %all-to-all-start.3 = ((f32[8,256,128]{1,2,0:T(8,128)}), f32[8,256,128]{1,2,0:T(8,128)S(1)}, u32[]{:S(2)}, u32[]{:S(2)}) async-start(f32[8,256,128]{1,2,0:T(8,128)} %broadcast_in_dim.24), calls=%async_computation.3 | async-start | bytes 2097152 | tf_op jit(solution)/shard_map/all_to_all | solution.py:17
  123.8 22.3 %all-to-all-start.2 = ((f32[8,256,128]{1,2,0:T(8,128)}), f32[8,256,128]{1,2,0:T(8,128)S(1)}, u32[]{:S(2)}, u32[]{:S(2)}) async-start(f32[8,256,128]{1,2,0:T(8,128)} %broadcast_in_dim.23), calls=%async_computation.2 | async-start | bytes 2097152 | tf_op jit(solution)/shard_map/all_to_all | solution.py:17
  127.3 144.4 %all-gather.7.cloned.1.call-start = ((), (), s32[]{:S(2)}) async-start(), calls=%async_computation.9 | async-start | bytes 3932160 | tf_op jit(solution)/shard_map/all_gather | solution.py:71
  200.5 5.7 %copy-start = (f32[1,768,384]{2,1,0:T(8,128)S(1)}, f32[1,768,384]{2,1,0:T(8,128)}, u32[]{:S(2)}) copy-start(f32[1,768,384]{2,1,0:T(8,128)} %param.4) | copy-start | bytes 3538948
Sparse Core Ops, SparseCore 0:
  64.6 52.6 all-gather.4
  119.4 98.2 all-gather.8
  219.7 51.9 all-gather.6
where the time goes:
time: 299 us
  waiting for transfers between devices  142 us (47%)
  blocking collectives  69.3 us (23%)
  starting transfers between devices  32.8 us (11%)
  matrix products  30.4 us (10%)
  between operations  13.3 us (4%)
  local copies, waits for them, and re-layouts  9.02 us (3%)
    all_to_all x3, blocking collectives, sent_to_all(): lax.all_to_all(jnp.broadcast_to(shard[None], (devices, *shard.shape)), ax...  69.3 us
    all_to_all x5, waiting for transfers between devices, sent_to_all(): lax.all_to_all(jnp.broadcast_to(shard[None], (devices, *shard.shape)), ax...  65.3 us
    all_gather x1, waiting for transfers between devices, local(): right_panel = lax.all_gather(carried, 'row', axis=0, tiled=True)  54.1 us
    dot_general x6, matrix products, panel_dot(): jnp.dot(piece, panel, precision=HIGH, preferred_element_type=jnp.float32)  30.4 us
    all_to_all x5, starting transfers between devices, sent_to_all(): lax.all_to_all(jnp.broadcast_to(shard[None], (devices, *shard.shape)), ax...  25 us
    ppermute x2, waiting for transfers between devices, swapped(): lax.ppermute(shard, axis, [(i, i ^ 1 << distance) for i in range(lax.axis...  11.9 us
    all_gather x1, waiting for transfers between devices, local(): lax.all_gather(own_ed, 'col', axis=1, tiled=True)  9.86 us
    ppermute x2, starting transfers between devices, swapped(): lax.ppermute(shard, axis, [(i, i ^ 1 << distance) for i in range(lax.axis...  7.65 us
  transfers between devices with their start and end apart: 10, of which 9 were waited for; matrix products, arithmetic and copies ran while one was open for 6% of the time, Pallas kernels for 0%

commit v1 on v0

--- a/solution.py
+++ b/solution.py
@@ -68,7 +68,9 @@
     carried = panel_dot(
         jnp.zeros(source.shape, jnp.float32), gathered_copies(inverse, "col", 1), source_panel
     )
-    right_panel = lax.all_gather(carried, "row", axis=0, tiled=True)
+    right_panel = jnp.concatenate(
+        lax.all_to_all(jnp.stack([carried] * lax.axis_size("row")), "row", 0, 0), axis=0
+    )
     zeros = jnp.zeros_like(own_ee)
     start_terms = jnp.concatenate(
         [jnp.where(is_even, own_ee, zeros), jnp.where(is_even, zeros, own_ee)], axis=1

time: 299 us -> 289 us (0.967)
  waiting for transfers between devices: 142 us -> 114 us
  starting transfers between devices: 32.8 us -> 42.7 us
  local copies, waits for them, and re-layouts: 9.02 us -> 15.5 us
    all_gather x1 -> x0, waiting for transfers between devices: 54.1 us -> none  [local(): right_panel = lax.all_gather(carried, 'row', axis=0, tiled=True)]
    all_to_all x0 -> x1, waiting for transfers between devices: none -> 28.4 us  [local(): lax.all_to_all(jnp.stack([carried] * lax.axis_size('row')), 'row', 0, 0)]
    all_to_all x0 -> x1, starting transfers between devices: none -> 10 us  [local(): lax.all_to_all(jnp.stack([carried] * lax.axis_size('row')), 'row', 0, 0)]
  transfers between devices with their start and end apart: 10 -> 10, of which waited for: 9 -> 9; matrix products, arithmetic and copies ran while one was open for 6% -> 8% of each run, Pallas kernels for 0% -> 0%
where the time goes in v1:
time: 289 us; the launch traced here: 288 us
  waiting for transfers between devices  114 us (39%)
  blocking collectives  67.8 us (23%)
  starting transfers between devices  42.7 us (15%)
  matrix products  30.6 us (11%)
  local copies, waits for them, and re-layouts  15.5 us (5%)
  between operations  13.6 us (5%)
  other arithmetic  3.79 us (1%)
    all_to_all x3, blocking collectives, sent_to_all(): lax.all_to_all(jnp.broadcast_to(shard[None], (devices, *shard.shape)), ax...  67.8 us
    all_to_all x5, waiting for transfers between devices, sent_to_all(): lax.all_to_all(jnp.broadcast_to(shard[None], (devices, *shard.shape)), ax...  63.9 us
    dot_general x6, matrix products, panel_dot(): jnp.dot(piece, panel, precision=HIGH, preferred_element_type=jnp.float32)  30.6 us
    all_to_all x1, waiting for transfers between devices, local(): lax.all_to_all(jnp.stack([carried] * lax.axis_size('row')), 'row', 0, 0)  28.4 us
    all_to_all x5, starting transfers between devices, sent_to_all(): lax.all_to_all(jnp.broadcast_to(shard[None], (devices, *shard.shape)), ax...  25 us
    ppermute x2, waiting for transfers between devices, swapped(): lax.ppermute(shard, axis, [(i, i ^ 1 << distance) for i in range(lax.axis...  11.9 us
    all_to_all x1, starting transfers between devices, local(): lax.all_to_all(jnp.stack([carried] * lax.axis_size('row')), 'row', 0, 0)  10 us
    all_gather x1, waiting for transfers between devices, local(): lax.all_gather(own_ed, 'col', axis=1, tiled=True)  8.93 us
  transfers between devices with their start and end apart: 10, of which 9 were waited for; matrix products, arithmetic and copies ran while one was open for 8% of the time, Pallas kernels for 0%

profile of v1, /device:TPU:1, one launch (start us, length us, event | category | flops | bytes accessed | tf_op | source)
XLA Modules:
  0.0 287.8 jit_solution(15438581099616706849)
XLA Ops:
  6.5 4.5 %collective-permute-start = (f32[256,128]{1,0:T(8,128)}, f32[256,128]{1,0:T(8,128)S(1)}, u32[]{:S(2)}, u32[]{:S(2)}) collective-permute-start(f32[256,128]{1,0:T(8,128)} %bitcast.55), channel_id=1, source_target_pairs={{0,32},{32,0},{64,96},{96,64},{128,160},{160,128},{192,224},{224,1... | collective-permute-start | bytes 393224 | tf_op jit(solution)/shard_map/ppermute | solution.py:27
  11.0 2.6 collective-permute-done
  13.8 17.0 %all_to_all.46 = f32[8,256,128]{1,2,0:T(8,128)S(1)} all-to-all(f32[8,256,128]{1,2,0:T(8,128)S(1)} %broadcast_in_dim.21), channel_id=1, replica_groups=mesh['box'=16,'row'=4,'col'=8] {'col'}, dimensions={0} | all-to-all | bytes 2097152 | tf_op jit(solution)/shard_map/all_to_all | solution.py:17
  30.8 1.2 broadcast_in_dim.29
  32.0 9.1 %all-to-all-start.7 = ((f32[4,256,384]{2,1,0:T(8,128)}), f32[4,256,384]{2,1,0:T(8,128)S(1)}, u32[]{:S(2)}, u32[]{:S(2)}) async-start(f32[4,256,384]{2,1,0:T(8,128)} %broadcast_in_dim.29), calls=%async_computation.7 | async-start | bytes 3145728 | tf_op jit(solution)/shard_map/all_to_all | solution.py:17
  41.1 3.2 %collective-permute-start.1 = (f32[256,384]{1,0:T(8,128)S(1)}, f32[256,384]{1,0:T(8,128)S(1)}, u32[]{:S(2)}, u32[]{:S(2)}) collective-permute-start(f32[256,384]{1,0:T(8,128)S(1)} %bitcast.54), channel_id=1, source_target_pairs={{0,32},{32,0},{64,96},{96,64},{128,160},{160,128},{192,224},{224,1... | collective-permute-start | bytes 1179656 | tf_op jit(solution)/shard_map/ppermute | solution.py:27
  44.3 9.4 %collective-permute-done.1 = f32[256,384]{1,0:T(8,128)S(1)} collective-permute-done((f32[256,384]{1,0:T(8,128)S(1)}, f32[256,384]{1,0:T(8,128)S(1)}, u32[]{:S(2)}, u32[]{:S(2)}) %collective-permute-start.1) | collective-permute-done | bytes 393248 | tf_op jit(solution)/shard_map/ppermute | solution.py:27
  53.6 8.0 %all-to-all-done.7 = f32[4,256,384]{2,1,0:T(8,128)S(1)} async-done(((f32[4,256,384]{2,1,0:T(8,128)}), f32[4,256,384]{2,1,0:T(8,128)S(1)}, u32[]{:S(2)}, u32[]{:S(2)}) %all-to-all-start.7) | async-done | bytes 1572896 | tf_op jit(solution)/shard_map/all_to_all | solution.py:17
  61.7 1.9 broadcast_select_fusion.1
  65.3 4.4 %all-to-all-start.1 = ((f32[4,256,128]{2,1,0:T(8,128)}), f32[4,256,128]{2,1,0:T(8,128)S(1)}, u32[]{:S(2)}, u32[]{:S(2)}) async-start(f32[4,256,128]{2,1,0:T(8,128)} %broadcast_in_dim.22), calls=%async_computation.1 | async-start | bytes 1048576 | tf_op jit(solution)/shard_map/all_to_all | solution.py:17
  69.8 9.3 %all-to-all-done.1 = f32[4,256,128]{2,1,0:T(8,128)S(1)} async-done(((f32[4,256,128]{2,1,0:T(8,128)}), f32[4,256,128]{2,1,0:T(8,128)S(1)}, u32[]{:S(2)}, u32[]{:S(2)}) %all-to-all-start.1) | async-done | bytes 524320 | tf_op jit(solution)/shard_map/all_to_all | solution.py:17
  79.1 1.8 convert_add_fusion
  81.7 4.4 %all-to-all-start.4 = ((f32[4,256,128]{2,1,0:T(8,128)}), f32[4,256,128]{2,1,0:T(8,128)S(1)}, u32[]{:S(2)}, u32[]{:S(2)}) async-start(f32[4,256,128]{2,1,0:T(8,128)} %broadcast_in_dim.25), calls=%async_computation.4 | async-start | bytes 1048576 | tf_op jit(solution)/shard_map/all_to_all | solution.py:17
  86.3 15.5 %all-to-all-done.4 = f32[4,256,128]{2,1,0:T(8,128)S(1)} async-done(((f32[4,256,128]{2,1,0:T(8,128)}), f32[4,256,128]{2,1,0:T(8,128)S(1)}, u32[]{:S(2)}, u32[]{:S(2)}) %all-to-all-start.4) | async-done | bytes 524320 | tf_op jit(solution)/shard_map/all_to_all | solution.py:17
  101.8 1.1 broadcast_in_dim.24
  102.8 3.6 %all-to-all-start.3 = ((f32[8,256,128]{1,2,0:T(8,128)}), f32[8,256,128]{1,2,0:T(8,128)S(1)}, u32[]{:S(2)}, u32[]{:S(2)}) async-start(f32[8,256,128]{1,2,0:T(8,128)} %broadcast_in_dim.24), calls=%async_computation.3 | async-start | bytes 2097152 | tf_op jit(solution)/shard_map/all_to_all | solution.py:17
  107.3 14.7 %all-to-all-done.3 = f32[8,256,128]{1,2,0:T(8,128)S(1)} async-done(((f32[8,256,128]{1,2,0:T(8,128)}), f32[8,256,128]{1,2,0:T(8,128)S(1)}, u32[]{:S(2)}, u32[]{:S(2)}) %all-to-all-start.3) | async-done | bytes 1048608 | tf_op jit(solution)/shard_map/all_to_all | solution.py:17
  123.0 3.6 %all-to-all-start.2 = ((f32[8,256,128]{1,2,0:T(8,128)}), f32[8,256,128]{1,2,0:T(8,128)S(1)}, u32[]{:S(2)}, u32[]{:S(2)}) async-start(f32[8,256,128]{1,2,0:T(8,128)} %broadcast_in_dim.23), calls=%async_computation.2 | async-start | bytes 2097152 | tf_op jit(solution)/shard_map/all_to_all | solution.py:17
  126.6 1.8 fusion.4
  128.4 16.3 %all-to-all-done.2 = f32[8,256,128]{1,2,0:T(8,128)S(1)} async-done(((f32[8,256,128]{1,2,0:T(8,128)}), f32[8,256,128]{1,2,0:T(8,128)S(1)}, u32[]{:S(2)}, u32[]{:S(2)}) %all-to-all-start.2) | async-done | bytes 1048608 | tf_op jit(solution)/shard_map/all_to_all | solution.py:17
  144.7 21.3 %all_to_all.47 = f32[4,256,128]{2,1,0:T(8,128)S(1)} all-to-all(f32[4,256,128]{2,1,0:T(8,128)S(1)} %broadcast_in_dim.26), channel_id=1, replica_groups=mesh['box'=16,'row'=4,'col'=8] {'row'}, dimensions={0} | all-to-all | bytes 1048576 | tf_op jit(solution)/shard_map/all_to_all | solution.py:17
  166.0 1.8 convolution_add_fusion
  168.0 29.6 %all_to_all.48 = f32[8,256,128]{1,2,0:T(8,128)S(1)} all-to-all(f32[8,256,128]{1,2,0:T(8,128)S(1)} %broadcast_in_dim.27), channel_id=1, replica_groups=mesh['box'=16,'row'=4,'col'=8] {'col'}, dimensions={0} | all-to-all | bytes 2097152 | tf_op jit(solution)/shard_map/all_to_all | solution.py:17
  197.6 4.7 %fusion.5 = f32[256,768]{1,0:T(8,128)S(1)} fusion(f32[256,1024]{0,1:T(8,128)S(1)} %bitcast.47, f32[1024,768]{1,0:T(8,128)} %all-gather.4.cloned.1.call-done), kind=kOutput, calls=%fused_computation.13 | convolution fusion | flops 2415919104 | bytes 4980736 | tf_op jit(solution)/shard_map/dot_general | solution.py:31
  202.3 1.9 stack.2
  204.2 10.0 %all-to-all-start.8 = ((f32[4,256,768]{2,1,0:T(8,128)}), f32[4,256,768]{2,1,0:T(8,128)S(1)}, u32[]{:S(2)}, u32[]{:S(2)}) async-start(f32[4,256,768]{2,1,0:T(8,128)} %stack.2), calls=%async_computation.8 | async-start | bytes 6291456 | tf_op jit(solution)/shard_map/all_to_all | solution.py:72
  214.3 2.7 copy.8
  216.9 2.8 select_bitcast_fusion.1
  219.7 8.9 %all-gather.6.cloned.1.call-done = f32[1,768,1024]{2,1,0:T(8,128)} async-done(((f32[1,768,128]{2,1,0:T(8,128)}), f32[1,768,1024]{2,1,0:T(8,128)}) %all-gather.6.cloned.1.call-update) | async-done | bytes 3145744 | tf_op jit(solution)/shard_map/all_gather | solution.py:78
  228.7 28.4 %all-to-all-done.8 = f32[4,256,768]{2,1,0:T(8,128)S(1)} async-done(((f32[4,256,768]{2,1,0:T(8,128)}), f32[4,256,768]{2,1,0:T(8,128)S(1)}, u32[]{:S(2)}, u32[]{:S(2)}) %all-to-all-start.8) | async-done | bytes 3145760 | tf_op jit(solution)/shard_map/all_to_all | solution.py:72
  257.0 18.6 %maximum_add_fusion = f32[768,768]{0,1:T(8,128)} fusion(f32[768,384]{0,1:T(8,128)} %get-tuple-element.6, f32[768,384]{0,1:T(8,128)} %get-tuple-element.5, f32[1024,768]{1,0:T(8,128)S(1)} %bitcast.42, f32[1,768,1024]{2,1,0:T(8,128)} %all-gather.6.cloned.1.call-done), kind=kOutput, calls=%fused_computation.2 | convolution fusion | flops 7248936960 | bytes 11010048 | tf_op jit(solution)/shard_map/dot_general | solution.py:31
  275.6 5.3 %copy.14 = f32[1,768,2,384]{3,2,1,0:T(2,128)} copy(f32[1,768,2,384]{1,3,2,0:T(8,128)} %bitcast.43) | data formatting | bytes 4718592 | tf_op jit(solution)/shard_map/reshape | solution.py:79
  (22 shorter events, 5.0 us)
Async XLA Ops:
  6.5 24.2 %copy-start = (f32[1,256,384]{2,1,0:T(8,128)S(1)}, f32[1,256,384]{2,1,0:T(8,128)}, u32[]{:S(2)}) copy-start(f32[1,256,384]{2,1,0:T(8,128)} %param.6) | copy-start | bytes 1179652
  6.5 7.0 %collective-permute-start = (f32[256,128]{1,0:T(8,128)}, f32[256,128]{1,0:T(8,128)S(1)}, u32[]{:S(2)}, u32[]{:S(2)}) collective-permute-start(f32[256,128]{1,0:T(8,128)} %bitcast.55), channel_id=1, source_target_pairs={{0,32},{32,0},{64,96},{96,64},{128,160},{160,128},{192,224},{224,1... | collective-permute-start | bytes 393224 | tf_op jit(solution)/shard_map/ppermute | solution.py:27
  32.0 29.6 %all-to-all-start.7 = ((f32[4,256,384]{2,1,0:T(8,128)}), f32[4,256,384]{2,1,0:T(8,128)S(1)}, u32[]{:S(2)}, u32[]{:S(2)}) async-start(f32[4,256,384]{2,1,0:T(8,128)} %broadcast_in_dim.29), calls=%async_computation.7 | async-start | bytes 3145728 | tf_op jit(solution)/shard_map/all_to_all | solution.py:17
  41.1 156.5 %all-gather.4.cloned.1.call-start = ((), (), s32[]{:S(2)}) async-start(), calls=%async_computation.9 | async-start | bytes 3932160 | tf_op jit(solution)/shard_map/all_gather | solution.py:67
  41.1 12.6 %collective-permute-start.1 = (f32[256,384]{1,0:T(8,128)S(1)}, f32[256,384]{1,0:T(8,128)S(1)}, u32[]{:S(2)}, u32[]{:S(2)}) collective-permute-start(f32[256,384]{1,0:T(8,128)S(1)} %bitcast.54), channel_id=1, source_target_pairs={{0,32},{32,0},{64,96},{96,64},{128,160},{160,128},{192,224},{224,1... | collective-permute-start | bytes 1179656 | tf_op jit(solution)/shard_map/ppermute | solution.py:27
  61.7 2.9 copy-start.1
  65.3 13.8 %all-to-all-start.1 = ((f32[4,256,128]{2,1,0:T(8,128)}), f32[4,256,128]{2,1,0:T(8,128)S(1)}, u32[]{:S(2)}, u32[]{:S(2)}) async-start(f32[4,256,128]{2,1,0:T(8,128)} %broadcast_in_dim.22), calls=%async_computation.1 | async-start | bytes 1048576 | tf_op jit(solution)/shard_map/all_to_all | solution.py:17
  81.7 20.0 %all-to-all-start.4 = ((f32[4,256,128]{2,1,0:T(8,128)}), f32[4,256,128]{2,1,0:T(8,128)S(1)}, u32[]{:S(2)}, u32[]{:S(2)}) async-start(f32[4,256,128]{2,1,0:T(8,128)} %broadcast_in_dim.25), calls=%async_computation.4 | async-start | bytes 1048576 | tf_op jit(solution)/shard_map/all_to_all | solution.py:17
  102.8 19.1 %all-to-all-start.3 = ((f32[8,256,128]{1,2,0:T(8,128)}), f32[8,256,128]{1,2,0:T(8,128)S(1)}, u32[]{:S(2)}, u32[]{:S(2)}) async-start(f32[8,256,128]{1,2,0:T(8,128)} %broadcast_in_dim.24), calls=%async_computation.3 | async-start | bytes 2097152 | tf_op jit(solution)/shard_map/all_to_all | solution.py:17
  106.4 122.3 %all-gather.6.cloned.1.call-start = ((), (), s32[]{:S(2)}) async-start(), calls=%async_computation.10 | async-start | bytes 3538944 | tf_op jit(solution)/shard_map/all_gather | solution.py:78
  123.0 21.7 %all-to-all-start.2 = ((f32[8,256,128]{1,2,0:T(8,128)}), f32[8,256,128]{1,2,0:T(8,128)S(1)}, u32[]{:S(2)}, u32[]{:S(2)}) async-start(f32[8,256,128]{1,2,0:T(8,128)} %broadcast_in_dim.23), calls=%async_computation.2 | async-start | bytes 2097152 | tf_op jit(solution)/shard_map/all_to_all | solution.py:17
  204.2 52.8 %all-to-all-start.8 = ((f32[4,256,768]{2,1,0:T(8,128)}), f32[4,256,768]{2,1,0:T(8,128)S(1)}, u32[]{:S(2)}, u32[]{:S(2)}) async-start(f32[4,256,768]{2,1,0:T(8,128)} %stack.2), calls=%async_computation.8 | async-start | bytes 6291456 | tf_op jit(solution)/shard_map/all_to_all | solution.py:72
Sparse Core Ops, SparseCore 0:
  64.6 53.5 all-gather.3
  120.2 108.4 all-gather.5
